TPU v7x, 32 devices: a whole 2x2x4 slice. The times are simulated.
32 devices in a mesh: dp: 4 (over x, core), expert: 8 (over z, y).
Axes of the slice: x: 2, y: 2, z: 4, core: 2. Of those that a mesh axis runs over, the one named last changes fastest.
Arguments:
- tokens: bfloat16 [128, 256, 1280], P(('dp', 'expert')), may hold values from -32 to 32
- slot_keys: bfloat16 [1280, 8], replicated, may hold values from -20 to 20
- logit_scale: float32 [1], replicated, may hold values from 8 to 16
- up_weight: bfloat16 [8, 1280, 5120], P('expert', None, 'dp'), may hold values from -0.15625 to 0.15625
- up_bias: bfloat16 [8, 5120], P('expert', 'dp'), may hold values from -3 to 3
- down_weight: bfloat16 [8, 5120, 1280], P('expert', 'dp'), may hold values from -0.078125 to 0.078125
- down_bias: bfloat16 [8, 1280], replicated, may hold values from -3 to 3
Outputs:
- mixed_out: bfloat16 [128, 256, 1280], P(('dp', 'expert'))
All inputs are finite; a program needn't handle non-finite values.
Results may differ from a plain program's by a relative error of at most 0.017.
Values may be sent and summed in bfloat16 or wider, within the bound.
A program may use at most 64 MiB of HBM per device.

v0:
```python
import jax
import jax.numpy as jnp
from jax import lax
from jax.sharding import PartitionSpec as P

norm_eps = 1e-06


def unit_rms(values, axis_pos):
    return values * lax.rsqrt(jnp.mean(values * values, axis=axis_pos, keepdims=True) + norm_eps)


def body(tokens, slot_keys, logit_scale, up_weight, up_bias, down_weight, down_bias):
    images = tokens.shape[0]
    patches = tokens.shape[1]
    width = tokens.shape[2]
    per_owner = up_weight.shape[0]
    owners = lax.axis_size("expert")
    normed_tok = unit_rms(tokens.astype(jnp.float32), 2).astype(jnp.bfloat16)
    normed_keys = unit_rms(slot_keys.astype(jnp.float32), 0).astype(jnp.bfloat16)
    raw_scores = jnp.einsum(
        "ipd,dn->inp", normed_tok, normed_keys, preferred_element_type=jnp.float32
    )
    logits = logit_scale[0] * raw_scores / width
    dispatch = jax.nn.softmax(logits, axis=2).astype(jnp.bfloat16)
    combine = jax.nn.softmax(logits, axis=1).astype(jnp.bfloat16)
    slot_inputs = jnp.einsum(
        "inp,ipd->ind", dispatch, tokens, preferred_element_type=jnp.float32
    ).astype(jnp.bfloat16)
    routed = lax.all_to_all(slot_inputs, "expert", split_axis=1, concat_axis=0, tiled=True)
    pre = jnp.einsum(
        "rkd,kdf->rkf",
        lax.all_gather(routed, "dp", axis=0, tiled=True),
        up_weight,
        preferred_element_type=jnp.float32,
    )
    pre = pre + up_bias.astype(jnp.float32)[None]
    hidden = jax.nn.gelu(pre, approximate=False).astype(jnp.bfloat16)
    summed = lax.psum_scatter(
        jnp.einsum("rkf,kfd->rkd", hidden, down_weight, preferred_element_type=jnp.float32).astype(
            jnp.bfloat16
        ),
        "dp",
        scatter_dimension=0,
        tiled=True,
    ).astype(jnp.float32)
    own_bias = lax.dynamic_slice_in_dim(
        down_bias, lax.axis_index("expert") * per_owner, per_owner, 0
    ).astype(jnp.float32)
    finished = (
        (summed + own_bias[None]).astype(jnp.bfloat16).reshape(owners, images, per_owner, width)
    )
    returned = lax.all_to_all(finished, "expert", split_axis=0, concat_axis=0, tiled=True)
    weights = combine.reshape(images, owners, per_owner, patches)
    mixed_out = jnp.einsum("iekp,eikd->ipd", weights, returned, preferred_element_type=jnp.float32)
    return mixed_out.astype(jnp.bfloat16)


def solution(mesh):
    return jax.shard_map(
        body,
        mesh=mesh,
        in_specs=(
            P(("dp", "expert"), None, None),
            P(),
            P(),
            P("expert", None, "dp"),
            P("expert", "dp"),
            P("expert", "dp", None),
            P(),
        ),
        out_specs=P(("dp", "expert"), None, None),
        check_vma=False,
    )
```

profile of v0, /device:TPU:0, one launch (start us, length us, event | category | flops | bytes accessed | tf_op | source)
XLA Modules:
  0.0 83.9 jit_solution(10107239753829949492)
XLA Ops:
  6.5 0.0 copy-start
  7.3 1.0 %fusion.96 = f32[8]{0:T(128)S(1)} fusion(bf16[1280,8]{0,1:T(8,128)(2,1)} %param.8), kind=kLoop, calls=%fused_computation.87 | loop fusion | flops 30712 | bytes 20512 | tf_op jit(solution)/shard_map/reduce_sum | solution.py:10
  8.4 2.3 %fusion.2 = f32[4,256]{1,0:T(4,128)S(1)} fusion(bf16[4,256,1280]{2,1,0:T(8,128)(2,1)} %param.7), kind=kLoop, calls=%fused_computation.4 | loop fusion | flops 3931136 | bytes 2625536 | tf_op jit(solution)/shard_map/reduce_sum | solution.py:10
  10.7 0.0 copy-start.1
  10.7 2.6 %fusion.33 = f32[4,8,256]{2,1,0:T(8,128)S(1)} fusion(bf16[4,256,1280]{2,1,0:T(8,128)(2,1)} %param.7, f32[4,256]{1,0:T(4,128)S(1)} %add_rsqrt_fusion, bf16[1280,8]{0,1:T(8,128)(2,1)} %param.8, f32[8]{0:T(128)S(1)} %add_rsqrt_fusion.1, f32[]{:T(128)} %bitcast.139), kind=kOutput, calls=%fused_computation.24 | convolution fusion | flops 24950784 | bytes 2678820 | tf_op jit(solution)/shard_map/ipd,dn->inp/dot_general | solution.py:21
  13.3 0.2 fusion.133
  13.5 2.2 %convolution_convert_fusion.1 = bf16[4,8,1280]{2,1,0:T(8,128)(2,1)S(1)} fusion(bf16[4,256,1280]{2,1,0:T(8,128)(2,1)} %param.7, f32[4,8]{1,0:T(4,128)S(1)} %fusion.133, f32[4,8,256]{2,1,0:T(8,128)S(1)} %fusion.33), kind=kOutput, calls=%fused_computation.17 | convolution fusion | flops 21037344 | bytes 2736256 | tf_op jit(solution)/shard_map/inp,ipd->ind/dot_general | solution.py:27
  15.8 0.7 copy.11
  16.4 7.3 %all-to-all-start = ((bf16[4,8,1280]{2,0,1:T(4,128)(2,1)}), bf16[4,8,1280]{2,0,1:T(4,128)(2,1)S(1)}, u32[]{:S(2)}, u32[]{:S(2)}) async-start(bf16[4,8,1280]{2,0,1:T(4,128)(2,1)} %copy.11), calls=%async_computation | async-start | bytes 163840 | tf_op jit(solution)/shard_map/all_to_all | solution.py:30
  23.7 0.0 reduce-scatter.2.cloned.1.call-start
  23.8 0.0 copy-done.1
  23.8 6.9 %all-to-all-done = bf16[4,8,1280]{2,0,1:T(4,128)(2,1)S(1)} async-done(((bf16[4,8,1280]{2,0,1:T(4,128)(2,1)}), bf16[4,8,1280]{2,0,1:T(4,128)(2,1)S(1)}, u32[]{:S(2)}, u32[]{:S(2)}) %all-to-all-start) | async-done | bytes 81952 | tf_op jit(solution)/shard_map/all_to_all | solution.py:30
  30.8 6.6 %all_gather.3 = bf16[128,1,1280]{2,0,1:T(8,128)(2,1)} all-gather(bf16[32,1,1280]{2,0,1:T(8,128)(2,1)S(1)} %all_to_all.19), channel_id=1, replica_groups=mesh['dp'=4,'expert'=8] {'dp'}, dimensions={0}, use_global_device_ids=true | all-gather | bytes 409600 | tf_op jit(solution)/shard_map/all_gather | solution.py:33
  37.3 0.0 copy-done
  37.3 5.2 %fusion.20 = bf16[128,1,1280]{2,0,1:T(8,128)(2,1)} fusion(bf16[1,1280,1280]{2,1,0:T(8,128)(2,1)S(1)} %copy-done, bf16[1,1280,1280]{2,1,0:T(8,128)(2,1)} %param.10, bf16[128,1,1280]{2,0,1:T(8,128)(2,1)} %all_gather.3, f32[1280]{0:T(1024)S(1)} %convert_reduce_fusion.1), kind=kOutput, calls=%fused_computation.16 | convolution fusion | flops 849838080 | bytes 7214080 | tf_op jit(solution)/shard_map/rkf,kfd->rkd/dot_general | solution.py:40
  42.6 0.0 reduce-scatter.2.cloned.1.call-update
  42.6 0.8 convert_reduce_fusion
  43.3 17.3 %reduce-scatter.2.cloned.1.call-done = bf16[32,1,1280]{2,0,1:T(8,128)(2,1)} async-done(((bf16[128,1,1280]{2,0,1:T(8,128)(2,1)}), bf16[32,1,1280]{2,0,1:T(8,128)(2,1)}) %reduce-scatter.2.cloned.1.call-update) | async-done | bytes 81936 | tf_op jit(solution)/shard_map/reduce_scatter | solution.py:39
  60.6 0.9 %add_convert_fusion = bf16[32,1,1280]{2,0,1:T(8,128)(2,1)S(1)} fusion(bf16[32,1,1280]{2,0,1:T(8,128)(2,1)} %reduce-scatter.2.cloned.1.call-done, f32[1280]{0:T(1024)S(1)} %convert_reduce_fusion), kind=kLoop, calls=%fused_computation.82 | loop fusion | flops 122880 | bytes 168960 | tf_op jit(solution)/shard_map/convert_element_type | solution.py:51
  61.5 0.7 reshape.56
  62.2 5.5 %all-to-all-start.1 = ((bf16[8,4,1,1280]{3,1,2,0:T(4,128)(2,1)}), bf16[8,4,1,1280]{3,1,2,0:T(4,128)(2,1)S(1)}, u32[]{:S(2)}, u32[]{:S(2)}) async-start(bf16[8,4,1,1280]{3,1,2,0:T(4,128)(2,1)} %bitcast.16), calls=%async_computation.2 | async-start | bytes 163840 | tf_op jit(solution)/shard_map/all_to_all | solution.py:53
  67.7 7.0 %all-to-all-done.1 = bf16[8,4,1,1280]{3,1,2,0:T(4,128)(2,1)S(1)} async-done(((bf16[8,4,1,1280]{3,1,2,0:T(4,128)(2,1)}), bf16[8,4,1,1280]{3,1,2,0:T(4,128)(2,1)S(1)}, u32[]{:S(2)}, u32[]{:S(2)}) %all-to-all-start.1) | async-done | bytes 81952 | tf_op jit(solution)/shard_map/all_to_all | solution.py:53
  74.7 2.4 %convolution_convert_fusion = bf16[4,256,1280]{2,1,0:T(8,128)(2,1)} fusion(bf16[8,4,1,1280]{3,1,2,0:T(4,128)(2,1)S(1)} %all-to-all-done.1, f32[4,256]{1,0:T(4,128)S(1)} %fusion.134, f32[4,8,256]{2,1,0:T(8,128)S(1)} %fusion.33), kind=kOutput, calls=%fused_computation.6 | convolution fusion | flops 22307848 | bytes 2740224 | tf_op jit(solution)/shard_map/iekp,eikd->ipd/dot_general | solution.py:55
  (5 shorter events, 0.1 us)
Async XLA Ops:
  6.5 30.8 %copy-start = (bf16[1,1280,1280]{2,1,0:T(8,128)(2,1)S(1)}, bf16[1,1280,1280]{2,1,0:T(8,128)(2,1)}, u32[]{:S(2)}) copy-start(bf16[1,1280,1280]{2,1,0:T(8,128)(2,1)} %param.12) | copy-start | bytes 9830404
  10.7 13.1 %copy-start.1 = (bf16[1,1280]{1,0:T(2,128)(2,1)S(1)}, bf16[1,1280]{1,0:T(2,128)(2,1)}, u32[]{:S(2)}) copy-start(bf16[1,1280]{1,0:T(2,128)(2,1)} %param.11) | copy-start | bytes 7684
  16.4 14.3 %all-to-all-start = ((bf16[4,8,1280]{2,0,1:T(4,128)(2,1)}), bf16[4,8,1280]{2,0,1:T(4,128)(2,1)S(1)}, u32[]{:S(2)}, u32[]{:S(2)}) async-start(bf16[4,8,1280]{2,0,1:T(4,128)(2,1)} %copy.11), calls=%async_computation | async-start | bytes 163840 | tf_op jit(solution)/shard_map/all_to_all | solution.py:30
  23.7 36.9 %reduce-scatter.2.cloned.1.call-start = ((), (), s32[]{:S(2)}) async-start(), calls=%async_computation.3 | async-start | bytes 409600 | tf_op jit(solution)/shard_map/reduce_scatter | solution.py:39
  62.2 12.5 %all-to-all-start.1 = ((bf16[8,4,1,1280]{3,1,2,0:T(4,128)(2,1)}), bf16[8,4,1,1280]{3,1,2,0:T(4,128)(2,1)S(1)}, u32[]{:S(2)}, u32[]{:S(2)}) async-start(bf16[8,4,1,1280]{3,1,2,0:T(4,128)(2,1)} %bitcast.16), calls=%async_computation.2 | async-start | bytes 163840 | tf_op jit(solution)/shard_map/all_to_all | solution.py:53
Sparse Core Ops, SparseCore 0:
  42.7 17.8 reduce-scatter.1
where the time goes:
time: 84.4 us; the launch traced here: 83.9 us
  waiting for transfers between devices  31.2 us (37%)
  between operations  14.2 us (17%)
  starting transfers between devices  12.8 us (15%)
  matrix products  12.5 us (15%)
  blocking collectives  6.55 us (8%)
  other arithmetic  5.26 us (6%)
  local copies, waits for them, and re-layouts  1.37 us (2%)
    reduce_scatter x1, waiting for transfers between devices, body(): lax.psum_scatter(jnp.einsum('rkf,kfd->rkd', hidden, down_weight, preferre...  17.3 us
    all_to_all x1, starting transfers between devices, body(): lax.all_to_all(slot_inputs, 'expert', split_axis=1, concat_axis=0, tiled=...  7.31 us
    all_to_all x1, waiting for transfers between devices, body(): lax.all_to_all(finished, 'expert', split_axis=0, concat_axis=0, tiled=True)  6.98 us
    all_to_all x1, waiting for transfers between devices, body(): lax.all_to_all(slot_inputs, 'expert', split_axis=1, concat_axis=0, tiled=...  6.93 us
    all_gather x1, blocking collectives, body(): lax.all_gather(routed, 'dp', axis=0, tiled=True)  6.55 us
    all_to_all x1, starting transfers between devices, body(): lax.all_to_all(finished, 'expert', split_axis=0, concat_axis=0, tiled=True)  5.5 us
    dot_general x1, matrix products, body(): jnp.einsum('rkf,kfd->rkd', hidden, down_weight, preferred_element_type=jn...  5.22 us
    reduce_sum x2, other arithmetic, unit_rms(): jnp.mean(values * values, axis=axis_pos, keepdims=True) + norm_eps  3.35 us
  transfers between devices with their start and end apart: 3, of which 3 were waited for; matrix products, arithmetic and copies ran while one was open for 1% of the time, Pallas kernels for 0%

commit v1 on v0

--- a/solution.py
+++ b/solution.py
@@ -4,6 +4,12 @@
 from jax.sharding import PartitionSpec as P
 
 norm_eps = 1e-06
+
+
+def in_order(blocks, dim):
+    blocks = jnp.moveaxis(blocks, 0, dim)
+    shape = blocks.shape
+    return blocks.reshape(*shape[:dim], shape[dim] * shape[dim + 1], *shape[dim + 2 :])
 
 
 def unit_rms(values, axis_pos):
@@ -28,12 +34,26 @@
         "inp,ipd->ind", dispatch, tokens, preferred_element_type=jnp.float32
     ).astype(jnp.bfloat16)
     routed = lax.all_to_all(slot_inputs, "expert", split_axis=1, concat_axis=0, tiled=True)
-    pre = jnp.einsum(
-        "rkd,kdf->rkf",
-        lax.all_gather(routed, "dp", axis=0, tiled=True),
-        up_weight,
-        preferred_element_type=jnp.float32,
-    )
+    size, index, width_2 = (lax.axis_size("dp"), lax.axis_index("dp"), routed.shape[0])
+    forward = [(i, (i + 1) % size) for i in range(size)]
+    backward = [(i, (i - 1) % size) for i in range(size)]
+    half = size // 2
+    blocks = {}
+    from_left = from_right = routed
+    for step in range(half + 1):
+        next_left = lax.ppermute(from_left, "dp", forward) if step < half else None
+        next_right = lax.ppermute(from_right, "dp", backward) if step < size - half - 1 else None
+        blocks[-step] = jnp.einsum(
+            "rkd,kdf->rkf", from_left, up_weight, preferred_element_type=jnp.float32
+        )
+        if 0 < step < size - half:
+            blocks[step] = jnp.einsum(
+                "rkd,kdf->rkf", from_right, up_weight, preferred_element_type=jnp.float32
+            )
+        from_left, from_right = (next_left, next_right)
+    blocks = jnp.stack([blocks[k] for k in sorted(blocks)])
+    blocks = blocks[(jnp.arange(size) - index + half) % size]
+    pre = in_order(blocks, 0)
     pre = pre + up_bias.astype(jnp.float32)[None]
     hidden = jax.nn.gelu(pre, approximate=False).astype(jnp.bfloat16)
     summed = lax.psum_scatter(

time: 84.4 us -> 90.8 us (1.076)
  blocking collectives: 6.55 us -> 0 us
  other arithmetic: 5.26 us -> 9.84 us
  waiting for transfers between devices: 31.2 us -> 35.4 us
  local copies, waits for them, and re-layouts: 1.37 us -> 4.03 us
    all_gather x1 -> x0, blocking collectives: 6.55 us -> none  [body(): lax.all_gather(routed, 'dp', axis=0, tiled=True)]
    ppermute x0 -> x3, waiting for transfers between devices: none -> 6.08 us  [the longest x2 6.08 us: body(): next_left = lax.ppermute(from_left, 'dp', forward) if step < half else None]
    convert_element_type x0 -> x2, other arithmetic: none -> 3.1 us  [the longest x1 2.51 us: body(): hidden = jax.nn.gelu(pre, approximate=False).astype(jnp.bfloat16)]
    dot_general x0 -> x4, matrix products: none -> 2.73 us  [the longest x3 2.04 us: body(): jnp.einsum('rkd,kdf->rkf', from_left, up_weight, preferred_element_type=j...]
    gather x0 -> x1, local copies, waits for them, and re-layouts: none -> 2.63 us  [body(): blocks = blocks[(jnp.arange(size) - index + half) % size]]
    dot_general x1, matrix products: 5.22 us -> 3.26 us  [body(): jnp.einsum('rkf,kfd->rkd', hidden, down_weight, preferred_element_type=jn...]
    all_to_all x1, waiting for transfers between devices: 6.93 us -> 5.75 us  [body(): lax.all_to_all(slot_inputs, 'expert', split_axis=1, concat_axis=0, tiled=...]
  transfers between devices with their start and end apart: 3 -> 6, of which waited for: 3 -> 5; matrix products, arithmetic and copies ran while one was open for 1% -> 4% of each run, Pallas kernels for 0% -> 0%
where the time goes in v1:
time: 90.8 us; the launch traced here: 90.2 us
  waiting for transfers between devices  35.4 us (39%)
  between operations  14.3 us (16%)
  starting transfers between devices  13.4 us (15%)
  matrix products  13.2 us (15%)
  other arithmetic  9.84 us (11%)
  local copies, waits for them, and re-layouts  4.03 us (4%)
    reduce_scatter x1, waiting for transfers between devices, body(): lax.psum_scatter(jnp.einsum('rkf,kfd->rkd', hidden, down_weight, preferre...  16.5 us
    all_to_all x1, starting transfers between devices, body(): lax.all_to_all(slot_inputs, 'expert', split_axis=1, concat_axis=0, tiled=...  7.31 us
    all_to_all x1, waiting for transfers between devices, body(): lax.all_to_all(finished, 'expert', split_axis=0, concat_axis=0, tiled=True)  6.98 us
    ppermute x2, waiting for transfers between devices, body(): next_left = lax.ppermute(from_left, 'dp', forward) if step < half else None  6.08 us
    all_to_all x1, waiting for transfers between devices, body(): lax.all_to_all(slot_inputs, 'expert', split_axis=1, concat_axis=0, tiled=...  5.75 us
    all_to_all x1, starting transfers between devices, body(): lax.all_to_all(finished, 'expert', split_axis=0, concat_axis=0, tiled=True)  5.53 us
    reduce_sum x2, other arithmetic, unit_rms(): jnp.mean(values * values, axis=axis_pos, keepdims=True) + norm_eps  3.35 us
    dot_general x1, matrix products, body(): jnp.einsum('rkf,kfd->rkd', hidden, down_weight, preferred_element_type=jn...  3.26 us
  transfers between devices with their start and end apart: 6, of which 5 were waited for; matrix products, arithmetic and copies ran while one was open for 4% of the time, Pallas kernels for 0%

profile of v1, /device:TPU:0, one launch (start us, length us, event | category | flops | bytes accessed | tf_op | source)
XLA Modules:
  0.0 90.2 jit_solution(12501815286602868935)
XLA Ops:
  6.5 0.0 copy-start
  7.3 1.0 %fusion.63 = f32[8]{0:T(128)S(1)} fusion(bf16[1280,8]{0,1:T(8,128)(2,1)} %param.8), kind=kLoop, calls=%fused_computation.63 | loop fusion | flops 30712 | bytes 20512 | tf_op jit(solution)/shard_map/reduce_sum | solution.py:16
  8.4 2.3 %fusion.2 = f32[4,256]{1,0:T(4,128)S(1)} fusion(bf16[4,256,1280]{2,1,0:T(8,128)(2,1)} %param.7), kind=kLoop, calls=%fused_computation.5 | loop fusion | flops 3931136 | bytes 2625536 | tf_op jit(solution)/shard_map/reduce_sum | solution.py:16
  10.7 0.0 copy-start.2
  10.7 2.6 %fusion.45 = f32[4,8,256]{2,1,0:T(8,128)S(1)} fusion(bf16[4,256,1280]{2,1,0:T(8,128)(2,1)} %param.7, f32[4,256]{1,0:T(4,128)S(1)} %add_rsqrt_fusion, bf16[1280,8]{0,1:T(8,128)(2,1)} %param.8, f32[8]{0:T(128)S(1)} %add_rsqrt_fusion.1, f32[]{:T(128)} %bitcast.106), kind=kOutput, calls=%fused_computation.33 | convolution fusion | flops 24950784 | bytes 2678820 | tf_op jit(solution)/shard_map/ipd,dn->inp/dot_general | solution.py:27
  13.3 0.2 fusion.72
  13.5 2.2 %convolution_convert_fusion.1 = bf16[4,8,1280]{2,1,0:T(8,128)(2,1)S(1)} fusion(bf16[4,256,1280]{2,1,0:T(8,128)(2,1)} %param.7, f32[4,8]{1,0:T(4,128)S(1)} %fusion.72, f32[4,8,256]{2,1,0:T(8,128)S(1)} %fusion.45), kind=kOutput, calls=%fused_computation.26 | convolution fusion | flops 21037344 | bytes 2736256 | tf_op jit(solution)/shard_map/inp,ipd->ind/dot_general | solution.py:33
  15.8 0.7 copy.12
  16.4 7.3 %all-to-all-start = ((bf16[4,8,1280]{2,0,1:T(4,128)(2,1)}), bf16[4,8,1280]{2,0,1:T(4,128)(2,1)S(1)}, u32[]{:S(2)}, u32[]{:S(2)}) async-start(bf16[4,8,1280]{2,0,1:T(4,128)(2,1)} %copy.12), calls=%async_computation | async-start | bytes 163840 | tf_op jit(solution)/shard_map/all_to_all | solution.py:36
  23.7 0.0 reduce-scatter.2.cloned.1.call-start
  23.8 0.6 pad_clamp_fusion
  24.4 0.0 copy-done.2
  24.4 0.6 convert_reduce_fusion.1
  25.0 5.8 %all-to-all-done = bf16[4,8,1280]{2,0,1:T(4,128)(2,1)S(1)} async-done(((bf16[4,8,1280]{2,0,1:T(4,128)(2,1)}), bf16[4,8,1280]{2,0,1:T(4,128)(2,1)S(1)}, u32[]{:S(2)}, u32[]{:S(2)}) %all-to-all-start) | async-done | bytes 81952 | tf_op jit(solution)/shard_map/all_to_all | solution.py:36
  30.8 0.1 collective-permute-start.2
  30.9 0.5 collective-permute-start
  31.4 0.0 copy-done
  31.4 0.7 fusion.29
  32.1 3.6 %collective-permute-done = bf16[32,1,1280]{2,0,1:T(8,128)(2,1)S(1)} collective-permute-done((bf16[32,1,1280]{2,0,1:T(8,128)(2,1)S(1)}, bf16[32,1,1280]{2,0,1:T(8,128)(2,1)S(1)}, u32[]{:S(2)}, u32[]{:S(2)}) %collective-permute-start) | collective-permute-done | bytes 81952 | tf_op jit(solution)/shard_map/ppermute | solution.py:44
  35.7 0.0 collective-permute-start.1
  35.7 0.7 fusion.26
  36.3 0.0 collective-permute-done.2
  36.3 0.7 fusion.32
  37.0 0.0 copy-start.1
  37.0 2.5 %collective-permute-done.1 = bf16[32,1,1280]{2,0,1:T(8,128)(2,1)S(1)} collective-permute-done((bf16[32,1,1280]{2,0,1:T(8,128)(2,1)S(1)}, bf16[32,1,1280]{2,0,1:T(8,128)(2,1)S(1)}, u32[]{:S(2)}, u32[]{:S(2)}) %collective-permute-start.1) | collective-permute-done | bytes 81952 | tf_op jit(solution)/shard_map/ppermute | solution.py:44
  39.5 0.7 fusion.23
  40.2 0.9 maximum_bitcast_fusion
  41.1 2.6 %gather_fusion = f32[4,32,1280]{2,1,0:T(8,128)} fusion(f32[4,32,1280]{2,1,0:T(8,128)} %maximum_bitcast_fusion, s32[1024]{0:T(1024)} %pad_clamp_fusion), kind=kCustom, calls=%fused_computation | custom fusion | bytes 1310736 | tf_op jit(solution)/shard_map/gather | solution.py:55
  43.7 0.0 copy-done.1
  43.7 2.5 %fusion.50 = bf16[4,32,1,1280]{3,1,0,2:T(8,128)(2,1)S(1)} fusion(f32[4,32,1280]{2,1,0:T(8,128)} %gather_fusion, f32[1280]{0:T(1024)S(1)} %copy-done.1), kind=kLoop, calls=%fused_computation.37 | loop fusion | flops 10813440 | bytes 988160 | tf_op jit(solution)/shard_map/convert_element_type | solution.py:58
  46.2 3.3 %fusion.20 = bf16[128,1,1280]{2,0,1:T(8,128)(2,1)} fusion(bf16[128,1280]{1,0:T(8,128)(2,1)S(1)} %bitcast.107, bf16[1,1280,1280]{2,1,0:T(8,128)(2,1)} %param.12), kind=kOutput, calls=%fused_computation.21 | convolution fusion | flops 419594240 | bytes 3932160 | tf_op jit(solution)/shard_map/rkf,kfd->rkd/dot_general | solution.py:60
  49.5 0.0 reduce-scatter.2.cloned.1.call-update
  49.5 0.8 convert_reduce_fusion
  50.3 16.5 %reduce-scatter.2.cloned.1.call-done = bf16[32,1,1280]{2,0,1:T(8,128)(2,1)} async-done(((bf16[128,1,1280]{2,0,1:T(8,128)(2,1)}), bf16[32,1,1280]{2,0,1:T(8,128)(2,1)}) %reduce-scatter.2.cloned.1.call-update) | async-done | bytes 81936 | tf_op jit(solution)/shard_map/reduce_scatter | solution.py:59
  66.8 0.9 %add_convert_fusion = bf16[32,1,1280]{2,0,1:T(8,128)(2,1)S(1)} fusion(bf16[32,1,1280]{2,0,1:T(8,128)(2,1)} %reduce-scatter.2.cloned.1.call-done, f32[1280]{0:T(1024)S(1)} %convert_reduce_fusion), kind=kLoop, calls=%fused_computation.55 | loop fusion | flops 122880 | bytes 168960 | tf_op jit(solution)/shard_map/convert_element_type | solution.py:71
  67.7 0.7 reshape.433
  68.4 5.5 %all-to-all-start.1 = ((bf16[8,4,1,1280]{3,1,2,0:T(4,128)(2,1)}), bf16[8,4,1,1280]{3,1,2,0:T(4,128)(2,1)S(1)}, u32[]{:S(2)}, u32[]{:S(2)}) async-start(bf16[8,4,1,1280]{3,1,2,0:T(4,128)(2,1)} %bitcast.34), calls=%async_computation.2 | async-start | bytes 163840 | tf_op jit(solution)/shard_map/all_to_all | solution.py:73
  73.9 7.0 %all-to-all-done.1 = bf16[8,4,1,1280]{3,1,2,0:T(4,128)(2,1)S(1)} async-done(((bf16[8,4,1,1280]{3,1,2,0:T(4,128)(2,1)}), bf16[8,4,1,1280]{3,1,2,0:T(4,128)(2,1)S(1)}, u32[]{:S(2)}, u32[]{:S(2)}) %all-to-all-start.1) | async-done | bytes 81952 | tf_op jit(solution)/shard_map/all_to_all | solution.py:73
  80.9 2.4 %convolution_convert_fusion = bf16[4,256,1280]{2,1,0:T(8,128)(2,1)} fusion(bf16[8,4,1,1280]{3,1,2,0:T(4,128)(2,1)S(1)} %all-to-all-done.1, f32[4,256]{1,0:T(4,128)S(1)} %fusion.73, f32[4,8,256]{2,1,0:T(8,128)S(1)} %fusion.45), kind=kOutput, calls=%fused_computation.7 | convolution fusion | flops 22307848 | bytes 2740224 | tf_op jit(solution)/shard_map/iekp,eikd->ipd/dot_general | solution.py:75
  (6 shorter events, 0.1 us)
Async XLA Ops:
  6.5 24.8 %copy-start = (bf16[1,1280,1280]{2,1,0:T(8,128)(2,1)S(1)}, bf16[1,1280,1280]{2,1,0:T(8,128)(2,1)}, u32[]{:S(2)}) copy-start(bf16[1,1280,1280]{2,1,0:T(8,128)(2,1)} %param.10) | copy-start | bytes 9830404
  10.7 13.7 %copy-start.2 = (bf16[1,1280]{1,0:T(2,128)(2,1)S(1)}, bf16[1,1280]{1,0:T(2,128)(2,1)}, u32[]{:S(2)}) copy-start(bf16[1,1280]{1,0:T(2,128)(2,1)} %param.11) | copy-start | bytes 7684
  16.4 14.3 %all-to-all-start = ((bf16[4,8,1280]{2,0,1:T(4,128)(2,1)}), bf16[4,8,1280]{2,0,1:T(4,128)(2,1)S(1)}, u32[]{:S(2)}, u32[]{:S(2)}) async-start(bf16[4,8,1280]{2,0,1:T(4,128)(2,1)} %copy.12), calls=%async_computation | async-start | bytes 163840 | tf_op jit(solution)/shard_map/all_to_all | solution.py:36
  23.7 43.1 %reduce-scatter.2.cloned.1.call-start = ((), (), s32[]{:S(2)}) async-start(), calls=%async_computation.3 | async-start | bytes 409600 | tf_op jit(solution)/shard_map/reduce_scatter | solution.py:59
  30.8 5.5 %collective-permute-start.2 = (bf16[32,1,1280]{2,0,1:T(8,128)(2,1)S(1)}, bf16[32,1,1280]{2,0,1:T(8,128)(2,1)S(1)}, u32[]{:S(2)}, u32[]{:S(2)}) collective-permute-start(bf16[32,1,1280]{2,0,1:T(8,128)(2,1)S(1)} %all_to_all.19), channel_id=1, source_target_pairs={{0,24},{8,0},{16,8},{24,16},{1,25},{9,1},{17,9},{25,17},{2,26},{10... | collective-permute-start | bytes 245768 | tf_op jit(solution)/shard_map/ppermute | solution.py:45
  30.9 4.8 %collective-permute-start = (bf16[32,1,1280]{2,0,1:T(8,128)(2,1)S(1)}, bf16[32,1,1280]{2,0,1:T(8,128)(2,1)S(1)}, u32[]{:S(2)}, u32[]{:S(2)}) collective-permute-start(bf16[32,1,1280]{2,0,1:T(8,128)(2,1)S(1)} %all_to_all.19), channel_id=1, source_target_pairs={{0,8},{8,16},{16,24},{24,0},{1,9},{9,17},{17,25},{25,1},{2,10},{10... | collective-permute-start | bytes 245768 | tf_op jit(solution)/shard_map/ppermute | solution.py:44
  35.7 3.9 %collective-permute-start.1 = (bf16[32,1,1280]{2,0,1:T(8,128)(2,1)S(1)}, bf16[32,1,1280]{2,0,1:T(8,128)(2,1)S(1)}, u32[]{:S(2)}, u32[]{:S(2)}) collective-permute-start(bf16[32,1,1280]{2,0,1:T(8,128)(2,1)S(1)} %collective-permute-done), channel_id=1, source_target_pairs={{0,8},{8,16},{16,24},{24,0},{1,9},{9,17},{17,25},{25,1},{2,10},{10... | collective-permute-start | bytes 245768 | tf_op jit(solution)/shard_map/ppermute | solution.py:44
  37.0 6.7 %copy-start.1 = (f32[1280]{0:T(1024)S(1)}, f32[1280]{0:T(1024)}, u32[]{:S(2)}) copy-start(f32[1280]{0:T(1024)} %convert_reduce_fusion.1) | copy-start | bytes 15364
  68.4 12.5 %all-to-all-start.1 = ((bf16[8,4,1,1280]{3,1,2,0:T(4,128)(2,1)}), bf16[8,4,1,1280]{3,1,2,0:T(4,128)(2,1)S(1)}, u32[]{:S(2)}, u32[]{:S(2)}) async-start(bf16[8,4,1,1280]{3,1,2,0:T(4,128)(2,1)} %bitcast.34), calls=%async_computation.2 | async-start | bytes 163840 | tf_op jit(solution)/shard_map/all_to_all | solution.py:73
Sparse Core Ops, SparseCore 0:
  49.6 17.1 reduce-scatter.1
